TPU v7x, 256 devices: a whole 4x4x8 slice. The times are simulated.
256 devices in a mesh: view: 8 (over x, core), gauss: 32 (over y, z).
Axes of the slice: x: 4, y: 4, z: 8, core: 2. Of those that a mesh axis runs over, the one named last changes fastest.
Arguments:
- means: float32 [3, 524288], P(None, 'gauss'), may hold values from -1 to 1
- scales: float32 [3, 524288], P(None, 'gauss'), may hold values from 0.05 to 0.6
- quats: float32 [4, 524288], P(None, 'gauss'), may hold values from -6 to 6
- attrs: float32 [49, 524288], P(None, 'gauss'), may hold values from -6 to 6
- grad_screen: float32 [32, 2, 524288], P('view', None, 'gauss'), may hold values from -6 to 6
- visible: int32 [32, 524288], P('view', 'gauss'), may hold values 0 or 1
- clone_mask: int32 [524288], P('gauss'), may hold values from 0 to 1, as said below
- rotation: float32 [32, 3, 3], P('view'), may hold values from -3.5 to 3.5
- shift: float32 [32, 3], P('view'), may hold values from 2 to 5
- focal: float32 [32], P('view'), may hold values from 1 to 4
Outputs:
- peak_stats: float32 [2, 524288], P(None, 'gauss')
- clones: float32 [61, 524288], P(None, 'gauss')
- clone_total: int32 [], replicated
Inputs may be any that keep to these rules, and one draw needn't show every extreme that they name: `clone_mask`: in every draw some shard of 16384 consecutive Gaussians has all of them marked.
All inputs are finite; a program needn't handle non-finite values. No bound on the sum of `visible` on one device may be relied on, other than what follows from the above.
Results may differ from a plain program's by a relative error of at most 0.0003.
Values sent between devices are 32-bit elements; how exact they have to be, the bound alone decides.
No kernel may reach another device: no remote copies, remote signals or barrier semaphores. Data moves between devices by JAX's collectives and lax.ppermute only.
A program may use at most 128 MiB of HBM per device.

v0:
```python
import jax
import jax.numpy as jnp
from jax import lax
from jax.sharding import PartitionSpec as P

G_DEV = 16384


def copy_for_each(x, axis):
    count = lax.axis_size(axis)
    return lax.all_to_all(jnp.broadcast_to(x[None], (count, *x.shape)), axis, 0, 0, tiled=True)


def of_everyone(x, axis):
    return copy_for_each(x, axis).max(axis=0)


def together(arrays, axis):
    vector, at, done = (jnp.concatenate([a.reshape(-1) for a in arrays]), 0, [])
    running = of_everyone(vector, axis)
    for a in arrays:
        done.append(running[at : at + a.size].reshape(a.shape))
        at += a.size
    return tuple(done)


def folded_in_pairs(pieces, combine):
    while len(jax.tree.leaves(pieces)[0]) > 1:
        pieces = jax.vmap(combine)(*(pieces[side::2] for side in (0, 1)))
    return pieces[0]


def prefix(x, axis, combine, identity):
    count, mine = (lax.axis_size(axis), lax.axis_index(axis))
    passed = jnp.arange(count) < mine

    def kept(part, zero, own):
        part = jnp.where(
            passed.reshape(-1, *(1 for _ in own.shape)), part, jnp.asarray(zero, own.dtype)
        )
        return part

    pieces = copy_for_each(x, axis)
    return folded_in_pairs(kept(pieces, identity, x), combine)


def of_everyone_2(x, axis):
    everything = copy_for_each(x, axis)
    return jnp.sum(everything, axis=0)


def quat_factor(scales, quats):
    inv = 1.0 / jnp.sqrt(jnp.sum(quats * quats, axis=0) + 0.25)
    w, x, y, z = (quats[0] * inv, quats[1] * inv, quats[2] * inv, quats[3] * inv)
    rq = [
        [1 - 2 * (y * y + z * z), 2 * (x * y - w * z), 2 * (x * z + w * y)],
        [2 * (x * y + w * z), 1 - 2 * (x * x + z * z), 2 * (y * z - w * x)],
        [2 * (x * z - w * y), 2 * (y * z + w * x), 1 - 2 * (x * x + y * y)],
    ]
    return [[rq[i][j] * scales[j] for j in range(3)] for i in range(3)]


def view_stats(means, factor, grad, seen, rot, trans, focal_v):
    point = [
        rot[i, 0] * means[0] + rot[i, 1] * means[1] + rot[i, 2] * means[2] + trans[i]
        for i in range(3)
    ]
    depth = jnp.maximum(point[2], 1.0)
    j00 = focal_v / depth
    j02 = -focal_v * point[0] / (depth * depth)
    j12 = -focal_v * point[1] / (depth * depth)
    first = [j00 * rot[0, j] + j02 * rot[2, j] for j in range(3)]
    second = [j00 * rot[1, j] + j12 * rot[2, j] for j in range(3)]
    prow = [sum((first[j] * factor[j][k] for j in range(3))) for k in range(3)]
    qrow = [sum((second[j] * factor[j][k] for j in range(3))) for k in range(3)]
    a_val = prow[0] ** 2 + prow[1] ** 2 + prow[2] ** 2 + 0.3
    c_val = qrow[0] ** 2 + qrow[1] ** 2 + qrow[2] ** 2 + 0.3
    b_val = prow[0] * qrow[0] + prow[1] * qrow[1] + prow[2] * qrow[2]
    half = 0.5 * (a_val - c_val)
    lam = 0.5 * (a_val + c_val) + jnp.sqrt(half * half + b_val * b_val + 0.01)
    seenf = seen.astype(jnp.float32)
    radius = 3.0 * jnp.sqrt(lam) * seenf
    gnorm = jnp.sqrt(grad[0] * grad[0] + grad[1] * grad[1]) * seenf
    return (gnorm, radius)


def add_ints(earlier, later):
    return earlier + later


def body(means, scales, quats, attrs, grad_screen, visible, clone_mask, rotation, shift, focal):
    factor = quat_factor(scales, quats)
    gmax = jnp.zeros(means.shape[1], jnp.float32)
    rmax = jnp.zeros(means.shape[1], jnp.float32)
    for v in range(grad_screen.shape[0]):
        gnorm, radius = view_stats(
            means, factor, grad_screen[v], visible[v], rotation[v], shift[v], focal[v]
        )
        gmax = jnp.maximum(gmax, gnorm)
        rmax = jnp.maximum(rmax, radius)
    gmax, rmax = together((gmax, rmax), "view")
    peak = jnp.stack([gmax, rmax])
    rows = jnp.concatenate([means, scales, quats, attrs, peak], axis=0)
    feat_rows = rows.shape[0]
    shards = lax.axis_size("gauss")
    cap_blk = G_DEV // 128
    count = jnp.sum(clone_mask)
    blocks = (count + 127) // 128
    offset = prefix(blocks, "gauss", add_ints, jnp.int32(0))
    summed = of_everyone_2(count.astype(jnp.float32), "gauss")
    total = summed.astype(jnp.int32)
    rank = jnp.cumsum(clone_mask) - 1
    where_to = jnp.where(clone_mask == 1, rank, cap_blk * 128)
    packed = (
        jnp.zeros((feat_rows, cap_blk * 128), jnp.float32).at[:, where_to].set(rows, mode="drop")
    )
    packed = packed.reshape(feat_rows, cap_blk, 128)
    per = (cap_blk + shards - 1) // shards
    target = jnp.arange(shards, dtype=jnp.int32)[:, None]
    within = jnp.arange(per, dtype=jnp.int32)[None, :]
    local_blk = (target - offset) % shards + within * shards
    valid = local_blk < blocks
    picked = jnp.minimum(local_blk, cap_blk - 1).reshape(-1)
    outgoing = packed[:, picked, :] * valid.reshape(1, -1, 1).astype(jnp.float32)
    outgoing = outgoing.reshape(feat_rows, shards, per, 128)
    slot_ids = (
        jnp.where(valid, (offset + local_blk) // shards, cap_blk)
        .astype(jnp.int32)
        .reshape(1, shards, per)
    )
    width = 128 // lax.axis_size("view")
    start = lax.axis_index("view") * width
    portion = lax.dynamic_slice_in_dim(outgoing, start, width, 3)
    arrived, slots_in = (
        lax.all_to_all(portion, "gauss", split_axis=1, concat_axis=1, tiled=True),
        lax.all_to_all(slot_ids, "gauss", split_axis=1, concat_axis=1, tiled=True),
    )
    arrived = arrived.reshape(feat_rows, shards * per, width)
    partial_place = (
        jnp.zeros((feat_rows, cap_blk, width), jnp.float32)
        .at[:, slots_in.reshape(-1)]
        .set(arrived, mode="drop")
    )
    placed = lax.all_gather(partial_place, "view", axis=2, tiled=True)
    clones = placed.reshape(feat_rows, cap_blk * 128)
    return (peak, clones, total)


def solution(mesh):
    return jax.shard_map(
        body,
        mesh=mesh,
        in_specs=(
            P(None, "gauss"),
            P(None, "gauss"),
            P(None, "gauss"),
            P(None, "gauss"),
            P("view", None, "gauss"),
            P("view", "gauss"),
            P("gauss"),
            P("view", None, None),
            P("view", None),
            P("view"),
        ),
        out_specs=(P(None, "gauss"), P(None, "gauss"), P()),
        check_vma=False,
    )
```

profile of v0, /device:TPU:1, one launch (start us, length us, event | category | flops | bytes accessed | tf_op | source)
XLA Modules:
  0.0 326.7 jit_solution(10295088173397887772)
XLA Ops:
  7.2 1.0 copy.37
  8.9 2.1 compare_select_fusion
  12.2 12.0 %all-to-all-start.1 = ((s32[32,1,1]{2,1,0:T(1,128)}), s32[32,1,1]{2,1,0:T(1,128)S(1)}, u32[]{:S(2)}, u32[]{:S(2)}) async-start(s32[32,1,1]{2,1,0:T(1,128)} %broadcast_in_dim.45), calls=%async_computation.1 | async-start | bytes 32768 | tf_op jit(solution)/shard_map/all_to_all | solution.py:11
  24.2 2.4 fusion.6
  26.7 1.1 multiply_reduce_fusion
  28.4 0.8 fusion.9
  29.9 1.8 fusion.11
  31.7 1.5 fusion.16
  33.8 7.2 %multiply_add_fusion.23 = (f32[1,16384]{1,0:T(1,128)S(1)}, f32[1,16384]{1,0:T(1,128)S(1)}, f32[1,16384]{1,0:T(1,128)S(1)}, f32[1,16384]{1,0:T(1,128)S(1)}) fusion(f32[]{:T(128)} %bitcast.13, f32[]{:T(128)} %bitcast.9, f32[]{:T(128)} %bitcast.16, f32[3,16384]{1,0:T(4,128)} %param.10, f32[]{:T(128)} %bitcast.15, f32[]{:T(128)} %bitcast.14, f32[]{:T(128)S(6)} %neg.16, ...), kind=kLoop, calls=%fused_computation.35 | loop fusion | flops 327680 | bytes 458792 | tf_op jit(solution)/shard_map/add | solution.py:72
  41.1 7.3 %multiply_add_fusion.22 = (f32[1,16384]{1,0:T(1,128)S(1)}, f32[1,16384]{1,0:T(1,128)S(1)}, f32[1,16384]{1,0:T(1,128)S(1)}, f32[1,16384]{1,0:T(1,128)S(1)}) fusion(f32[1,16384]{1,0:T(1,128)S(1)} %get-tuple-element.22, f32[1,16384]{1,0:T(1,128)S(1)} %get-tuple-element.23, f32[]{:T(128)} %bitcast.14, f32[]{:T(128)} %bitcast.10, f32[]{:T(128)} %bitcast.11, ...), kind=kLoop, calls=%fused_computation.34 | loop fusion | flops 294912 | bytes 655400 | tf_op jit(solution)/shard_map/add | solution.py:72
  48.3 2.5 multiply_add_fusion.19
  52.2 7.4 %multiply_add_fusion.17 = (f32[1,16384]{1,0:T(1,128)S(1)}, f32[1,16384]{1,0:T(1,128)S(1)}, f32[1,16384]{1,0:T(1,128)S(1)}, f32[1,16384]{1,0:T(1,128)S(1)}) fusion(f32[]{:T(128)} %bitcast.39, f32[]{:T(128)} %bitcast.35, f32[]{:T(128)} %bitcast.42, f32[3,16384]{1,0:T(4,128)} %param.10, f32[]{:T(128)} %bitcast.41, f32[]{:T(128)} %bitcast.40, f32[]{:T(128)S(6)} %neg.17, ...), kind=kLoop, calls=%fused_computation.29 | loop fusion | flops 327680 | bytes 458792 | tf_op jit(solution)/shard_map/add | solution.py:72
  59.6 7.2 %multiply_add_fusion.16 = (f32[1,16384]{1,0:T(1,128)S(1)}, f32[1,16384]{1,0:T(1,128)S(1)}, f32[1,16384]{1,0:T(1,128)S(1)}, f32[1,16384]{1,0:T(1,128)S(1)}) fusion(f32[1,16384]{1,0:T(1,128)S(1)} %get-tuple-element.28, f32[1,16384]{1,0:T(1,128)S(1)} %get-tuple-element.29, f32[]{:T(128)} %bitcast.40, f32[]{:T(128)} %bitcast.36, f32[]{:T(128)} %bitcast.37, ...), kind=kLoop, calls=%fused_computation.28 | loop fusion | flops 294912 | bytes 655400 | tf_op jit(solution)/shard_map/add | solution.py:72
  66.8 2.5 multiply_add_fusion.13
  70.7 7.4 %multiply_add_fusion.11 = (f32[1,16384]{1,0:T(1,128)S(1)}, f32[1,16384]{1,0:T(1,128)S(1)}, f32[1,16384]{1,0:T(1,128)S(1)}, f32[1,16384]{1,0:T(1,128)S(1)}) fusion(f32[]{:T(128)} %bitcast.58, f32[]{:T(128)} %bitcast.54, f32[]{:T(128)} %bitcast.61, f32[3,16384]{1,0:T(4,128)} %param.10, f32[]{:T(128)} %bitcast.60, f32[]{:T(128)} %bitcast.59, f32[]{:T(128)S(6)} %neg.18, ...), kind=kLoop, calls=%fused_computation.23 | loop fusion | flops 327680 | bytes 458792 | tf_op jit(solution)/shard_map/add | solution.py:72
  78.1 7.4 %multiply_add_fusion.10 = (f32[1,16384]{1,0:T(1,128)S(1)}, f32[1,16384]{1,0:T(1,128)S(1)}, f32[1,16384]{1,0:T(1,128)S(1)}, f32[1,16384]{1,0:T(1,128)S(1)}) fusion(f32[1,16384]{1,0:T(1,128)S(1)} %get-tuple-element.34, f32[1,16384]{1,0:T(1,128)S(1)} %get-tuple-element.35, f32[]{:T(128)} %bitcast.59, f32[]{:T(128)} %bitcast.55, f32[]{:T(128)} %bitcast.56, ...), kind=kLoop, calls=%fused_computation.22 | loop fusion | flops 294912 | bytes 655400 | tf_op jit(solution)/shard_map/add | solution.py:72
  85.4 2.6 multiply_add_fusion.7
  89.4 7.4 %multiply_add_fusion.5 = (f32[1,16384]{1,0:T(1,128)S(1)}, f32[1,16384]{1,0:T(1,128)S(1)}, f32[1,16384]{1,0:T(1,128)S(1)}, f32[1,16384]{1,0:T(1,128)S(1)}) fusion(f32[]{:T(128)} %bitcast.77, f32[]{:T(128)} %bitcast.73, f32[]{:T(128)} %bitcast.80, f32[3,16384]{1,0:T(4,128)} %param.10, f32[]{:T(128)} %bitcast.79, f32[]{:T(128)} %bitcast.78, f32[]{:T(128)S(6)} %neg.19, ...), kind=kLoop, calls=%fused_computation.17 | loop fusion | flops 327680 | bytes 458792 | tf_op jit(solution)/shard_map/add | solution.py:72
  96.8 7.4 %multiply_add_fusion.4 = (f32[1,16384]{1,0:T(1,128)S(1)}, f32[1,16384]{1,0:T(1,128)S(1)}, f32[1,16384]{1,0:T(1,128)S(1)}, f32[1,16384]{1,0:T(1,128)S(1)}) fusion(f32[1,16384]{1,0:T(1,128)S(1)} %get-tuple-element.40, f32[1,16384]{1,0:T(1,128)S(1)} %get-tuple-element.41, f32[]{:T(128)} %bitcast.78, f32[]{:T(128)} %bitcast.74, f32[]{:T(128)} %bitcast.75, ...), kind=kLoop, calls=%fused_computation.16 | loop fusion | flops 294912 | bytes 655400 | tf_op jit(solution)/shard_map/add | solution.py:72
  104.2 2.6 multiply_add_fusion.1
  106.7 1.8 slice_convert_fusion.3
  108.5 0.8 fusion.7
  109.3 0.8 add_sqrt_fusion.3
  110.2 1.8 multiply_maximum_fusion
  112.0 1.5 broadcast_in_dim.24
  113.5 5.3 %all-to-all-start = ((f32[8,1,32768]{2,1,0:T(1,128)}), f32[8,1,32768]{2,1,0:T(1,128)S(1)}, u32[]{:S(2)}, u32[]{:S(2)}) async-start(f32[8,1,32768]{2,1,0:T(1,128)} %broadcast_in_dim.24), calls=%async_computation | async-start | bytes 2097152 | tf_op jit(solution)/shard_map/all_to_all | solution.py:11
  122.2 0.7 add_minimum_fusion
  123.0 0.7 fusion.2
  123.8 1.4 compare_select_fusion.1
  125.2 8.5 %all-to-all-done = f32[8,1,32768]{2,1,0:T(1,128)S(1)} async-done(((f32[8,1,32768]{2,1,0:T(1,128)}), f32[8,1,32768]{2,1,0:T(1,128)S(1)}, u32[]{:S(2)}, u32[]{:S(2)}) %all-to-all-start) | async-done | bytes 1048608 | tf_op jit(solution)/shard_map/all_to_all | solution.py:11
  133.7 9.7 %all-to-all-start.2 = ((s32[1,32,4]{2,0,1:T(1,128)}), s32[1,32,4]{2,0,1:T(1,128)S(1)}, u32[]{:S(2)}, u32[]{:S(2)}) async-start(s32[1,32,4]{2,0,1:T(1,128)} %compare_select_fusion.1), calls=%async_computation.2 | async-start | bytes 32768 | tf_op jit(solution)/shard_map/all_to_all | solution.py:136
  143.4 0.8 reduce_max.9
  144.2 21.5 %concatenate.8 = f32[61,16384]{1,0:T(8,128)} concatenate(f32[3,16384]{1,0:T(4,128)S(1)} %copy-done.1, f32[3,16384]{1,0:T(4,128)S(1)} %copy-done.3, f32[4,16384]{1,0:T(4,128)S(1)} %copy-done.2, f32[49,16384]{1,0:T(8,128)} %param.13, f32[1,16384]{1,0:T(1,128)S(1)} %bitcast.129, f32[1,16384]{1,0:T(1,128)S(1)} %bitcast.131), dimensions={0} | concatenate | bytes 7995392 | tf_op jit(solution)/shard_map/concatenate | solution.py:103
  165.8 6.9 %copy.40 = f32[16384,61]{1,0:T(8,128)} copy(f32[16384,61]{0,1:T(8,128)} %bitcast.126) | data formatting | bytes 7995392 | tf_op jit(solution)/shard_map/concatenate | solution.py:103
  172.7 44.3 %scatter_custom_fusion = f32[61,16384]{0,1:T(8,128)} fusion(s32[16384]{0:T(1024)} %get-tuple-element.78, f32[16384,61]{1,0:T(8,128)} %copy.40, f32[]{:T(128)} %constant.32.clone.1), kind=kCustom, calls=%fused_computation.3 | custom fusion | bytes 3998208 | tf_op jit(solution)/shard_map/scatter | solution.py:115
  217.0 7.7 %gather_fusion = f32[128,61,128]{1,2,0:T(8,128)} fusion(f32[61,128,128]{0,2,1:T(8,128)} %bitcast.125, s32[1024]{0:T(1024)S(1)} %pad_clamp_fusion), kind=kCustom, calls=%fused_computation | custom fusion | bytes 7995904 | tf_op jit(solution)/shard_map/gather | solution.py:124
  224.7 1.4 fusion.17
  226.2 2.3 reshape.640
  228.5 9.1 %all-to-all-start.3 = ((f32[32,1,3904]{2,1,0:T(1,128)}), f32[32,1,3904]{2,1,0:T(1,128)S(1)}, u32[]{:S(2)}, u32[]{:S(2)}) async-start(f32[32,1,3904]{2,1,0:T(1,128)} %reshape.640), calls=%async_computation.3 | async-start | bytes 1015808 | tf_op jit(solution)/shard_map/all_to_all | solution.py:135
  238.9 11.3 %all-to-all-done.3 = f32[32,1,3904]{2,1,0:T(1,128)S(1)} async-done(((f32[32,1,3904]{2,1,0:T(1,128)}), f32[32,1,3904]{2,1,0:T(1,128)S(1)}, u32[]{:S(2)}, u32[]{:S(2)}) %all-to-all-start.3) | async-done | bytes 499744 | tf_op jit(solution)/shard_map/all_to_all | solution.py:135
  250.8 1.8 reduce.9
  252.6 1.5 reshape.641
  254.2 4.5 %scatter_fusion = f32[61,128,16]{0,2,1:T(8,128)S(1)} fusion(f32[61,128,16]{0,2,1:T(8,128)S(1)} %broadcast_in_dim.44, s32[128]{0:T(128)S(1)} %fusion.4, f32[128,61,16]{1,2,0:T(8,128)S(1)} %bitcast.124), kind=kCustom, calls=%fused_computation.2 | custom fusion | bytes 1499648 | tf_op jit(solution)/shard_map/scatter | solution.py:142
  258.8 1.0 copy-done
  260.3 16.9 %all_to_all.31 = f32[32,1,1]{2,1,0:T(1,128)S(1)} all-to-all(f32[32,1,1]{2,1,0:T(1,128)S(1)} %broadcast_in_dim.51), channel_id=1, replica_groups=mesh['view'=8,'gauss'=32] {'gauss'}, dimensions={0} | all-to-all | bytes 256 | tf_op jit(solution)/shard_map/all_to_all | solution.py:11
  278.5 0.8 pad_maximum_fusion.1
  279.3 32.5 %all-gather.2.cloned.1.call-done = f32[61,128,128]{0,2,1:T(8,128)} async-done(((f32[61,128,16]{0,2,1:T(8,128)}), f32[61,128,128]{0,2,1:T(8,128)}) %all-gather.2.cloned.1.call-update) | async-done | bytes 3997712 | tf_op jit(solution)/shard_map/all_gather | solution.py:144
  311.8 6.8 %copy.42 = f32[61,16384]{1,0:T(8,128)} copy(f32[61,16384]{0,1:T(8,128)} %bitcast.127) | data formatting | bytes 7995392
  (58 shorter events, 9.4 us)
Async XLA Ops:
  7.2 101.4 %copy-start.3 = (f32[3,16384]{1,0:T(4,128)S(1)}, f32[3,16384]{1,0:T(4,128)}, u32[]{:S(2)}) copy-start(f32[3,16384]{1,0:T(4,128)} %param.11) | copy-start | bytes 589828
  7.2 102.1 %copy-start.4 = (f32[4,2,16384]{2,1,0:T(2,128)S(1)}, f32[4,2,16384]{2,1,0:T(2,128)}, u32[]{:S(2)}) copy-start(f32[4,2,16384]{2,1,0:T(2,128)} %param.14) | copy-start | bytes 1572868
  12.2 99.8 %all-to-all-start.1 = ((s32[32,1,1]{2,1,0:T(1,128)}), s32[32,1,1]{2,1,0:T(1,128)S(1)}, u32[]{:S(2)}, u32[]{:S(2)}) async-start(s32[32,1,1]{2,1,0:T(1,128)} %broadcast_in_dim.45), calls=%async_computation.1 | async-start | bytes 32768 | tf_op jit(solution)/shard_map/all_to_all | solution.py:11
  24.2 120.0 %copy-start.1 = (f32[3,16384]{1,0:T(4,128)S(1)}, f32[3,16384]{1,0:T(4,128)}, u32[]{:S(2)}) copy-start(f32[3,16384]{1,0:T(4,128)} %param.10) | copy-start | bytes 589828
  24.2 120.0 %copy-start.2 = (f32[4,16384]{1,0:T(4,128)S(1)}, f32[4,16384]{1,0:T(4,128)}, u32[]{:S(2)}) copy-start(f32[4,16384]{1,0:T(4,128)} %param.12) | copy-start | bytes 786436
  113.5 20.2 %all-to-all-start = ((f32[8,1,32768]{2,1,0:T(1,128)}), f32[8,1,32768]{2,1,0:T(1,128)S(1)}, u32[]{:S(2)}, u32[]{:S(2)}) async-start(f32[8,1,32768]{2,1,0:T(1,128)} %broadcast_in_dim.24), calls=%async_computation | async-start | bytes 2097152 | tf_op jit(solution)/shard_map/all_to_all | solution.py:11
  133.7 94.8 %all-to-all-start.2 = ((s32[1,32,4]{2,0,1:T(1,128)}), s32[1,32,4]{2,0,1:T(1,128)S(1)}, u32[]{:S(2)}, u32[]{:S(2)}) async-start(s32[1,32,4]{2,0,1:T(1,128)} %compare_select_fusion.1), calls=%async_computation.2 | async-start | bytes 32768 | tf_op jit(solution)/shard_map/all_to_all | solution.py:136
  228.5 21.8 %all-to-all-start.3 = ((f32[32,1,3904]{2,1,0:T(1,128)}), f32[32,1,3904]{2,1,0:T(1,128)S(1)}, u32[]{:S(2)}, u32[]{:S(2)}) async-start(f32[32,1,3904]{2,1,0:T(1,128)} %reshape.640), calls=%async_computation.3 | async-start | bytes 1015808 | tf_op jit(solution)/shard_map/all_to_all | solution.py:135
  237.6 74.3 %all-gather.2.cloned.1.call-start = ((), (), s32[]{:S(2)}) async-start(), calls=%async_computation.5 | async-start | bytes 9437184 | tf_op jit(solution)/shard_map/all_gather | solution.py:144
  258.8 1.0 copy-start
Sparse Core Ops, SparseCore 0:
  259.9 51.9 all-gather.1
where the time goes:
time: 329 us; the launch traced here: 327 us
  local copies, waits for them, and re-layouts  113 us (34%)
  other arithmetic  87.1 us (26%)
  waiting for transfers between devices  52.4 us (16%)
  starting transfers between devices  36.1 us (11%)
  between operations  21.3 us (6%)
  blocking collectives  16.9 us (5%)
    add x8, other arithmetic, view_stats(): first = [j00 * rot[0, j] + j02 * rot[2, j] for j in range(3)]  58.6 us
    scatter x1, local copies, waits for them, and re-layouts, body(): jnp.zeros((feat_rows, cap_blk * 128), jnp.float32).at[:, where_to]  44.3 us
    all_gather x1, waiting for transfers between devices, body(): placed = lax.all_gather(partial_place, 'view', axis=2, tiled=True)  32.5 us
    concatenate x2, local copies, waits for them, and re-layouts, body(): rows = jnp.concatenate([means, scales, quats, attrs, peak], axis=0)  28.5 us
    all_to_all x2, starting transfers between devices, copy_for_each(): lax.all_to_all(jnp.broadcast_to(x[None], (count, *x.shape)), axis, 0, 0,...  17.3 us
    all_to_all x1, blocking collectives, copy_for_each(): lax.all_to_all(jnp.broadcast_to(x[None], (count, *x.shape)), axis, 0, 0,...  16.9 us
    unnamed x15, local copies, waits for them, and re-layouts  11.7 us
    all_to_all x1, waiting for transfers between devices, body(): lax.all_to_all(portion, 'gauss', split_axis=1, concat_axis=1, tiled=True)  11.3 us
  transfers between devices with their start and end apart: 5, of which 3 were waited for; matrix products, arithmetic and copies ran while one was open for 54% of the time, Pallas kernels for 0%

commit v1 on v0

--- a/solution.py
+++ b/solution.py
@@ -4,6 +4,12 @@
 from jax.sharding import PartitionSpec as P
 
 G_DEV = 16384
+
+
+def exchange_blocks(shard, axis, split, join):
+    shards = jnp.split(shard, lax.axis_size(axis), axis=split)
+    got = lax.all_to_all(jnp.stack(shards), axis, 0, 0)
+    return jnp.concatenate(got, axis=join)
 
 
 def copy_for_each(x, axis):
@@ -132,7 +138,7 @@
     start = lax.axis_index("view") * width
     portion = lax.dynamic_slice_in_dim(outgoing, start, width, 3)
     arrived, slots_in = (
-        lax.all_to_all(portion, "gauss", split_axis=1, concat_axis=1, tiled=True),
+        exchange_blocks(portion, "gauss", 1, 1),
         lax.all_to_all(slot_ids, "gauss", split_axis=1, concat_axis=1, tiled=True),
     )
     arrived = arrived.reshape(feat_rows, shards * per, width)

time: 329 us -> 330 us (level)
    unnamed x15 -> x46, local copies, waits for them, and re-layouts: 11.7 us -> 11.8 us
where the time goes in v1:
time: 330 us; the launch traced here: 327 us
  local copies, waits for them, and re-layouts  113 us (34%)
  other arithmetic  87.2 us (26%)
  waiting for transfers between devices  52.4 us (16%)
  starting transfers between devices  36.1 us (11%)
  between operations  21.5 us (7%)
  blocking collectives  16.9 us (5%)
    add x8, other arithmetic, view_stats(): first = [j00 * rot[0, j] + j02 * rot[2, j] for j in range(3)]  58.6 us
    scatter x1, local copies, waits for them, and re-layouts, body(): jnp.zeros((feat_rows, cap_blk * 128), jnp.float32).at[:, where_to]  44.3 us
    all_gather x1, waiting for transfers between devices, body(): placed = lax.all_gather(partial_place, 'view', axis=2, tiled=True)  32.5 us
    concatenate x2, local copies, waits for them, and re-layouts, body(): rows = jnp.concatenate([means, scales, quats, attrs, peak], axis=0)  28.5 us
    all_to_all x2, starting transfers between devices, copy_for_each(): lax.all_to_all(jnp.broadcast_to(x[None], (count, *x.shape)), axis, 0, 0,...  17.3 us
    all_to_all x1, blocking collectives, copy_for_each(): lax.all_to_all(jnp.broadcast_to(x[None], (count, *x.shape)), axis, 0, 0,...  16.9 us
    unnamed x46, local copies, waits for them, and re-layouts  11.8 us
    all_to_all x1, waiting for transfers between devices, exchange_blocks(): got = lax.all_to_all(jnp.stack(shards), axis, 0, 0)  11.3 us
  transfers between devices with their start and end apart: 5, of which 3 were waited for; matrix products, arithmetic and copies ran while one was open for 54% of the time, Pallas kernels for 0%

profile of v1, /device:TPU:1, one launch (start us, length us, event | category | flops | bytes accessed | tf_op | source)
XLA Modules:
  0.0 327.1 jit_solution(16063473621375712980)
XLA Ops:
  7.2 1.0 copy.99
  8.9 2.1 compare_select_fusion
  12.2 12.0 %all-to-all-start.1 = ((s32[32,1,1]{2,1,0:T(1,128)}), s32[32,1,1]{2,1,0:T(1,128)S(1)}, u32[]{:S(2)}, u32[]{:S(2)}) async-start(s32[32,1,1]{2,1,0:T(1,128)} %broadcast_in_dim.45), calls=%async_computation.1 | async-start | bytes 32768 | tf_op jit(solution)/shard_map/all_to_all | solution.py:17
  24.2 2.4 fusion.6
  26.7 1.1 multiply_reduce_fusion
  28.4 0.8 fusion.9
  29.9 1.8 fusion.11
  31.7 1.5 fusion.16
  33.8 7.2 %multiply_add_fusion.23 = (f32[1,16384]{1,0:T(1,128)S(1)}, f32[1,16384]{1,0:T(1,128)S(1)}, f32[1,16384]{1,0:T(1,128)S(1)}, f32[1,16384]{1,0:T(1,128)S(1)}) fusion(f32[]{:T(128)} %bitcast.13, f32[]{:T(128)} %bitcast.9, f32[]{:T(128)} %bitcast.16, f32[3,16384]{1,0:T(4,128)} %param.10, f32[]{:T(128)} %bitcast.15, f32[]{:T(128)} %bitcast.14, f32[]{:T(128)S(6)} %neg.16, ...), kind=kLoop, calls=%fused_computation.67 | loop fusion | flops 327680 | bytes 458792 | tf_op jit(solution)/shard_map/add | solution.py:78
  41.1 7.3 %multiply_add_fusion.22 = (f32[1,16384]{1,0:T(1,128)S(1)}, f32[1,16384]{1,0:T(1,128)S(1)}, f32[1,16384]{1,0:T(1,128)S(1)}, f32[1,16384]{1,0:T(1,128)S(1)}) fusion(f32[1,16384]{1,0:T(1,128)S(1)} %get-tuple-element.22, f32[1,16384]{1,0:T(1,128)S(1)} %get-tuple-element.23, f32[]{:T(128)} %bitcast.14, f32[]{:T(128)} %bitcast.10, f32[]{:T(128)} %bitcast.11, ...), kind=kLoop, calls=%fused_computation.66 | loop fusion | flops 294912 | bytes 655400 | tf_op jit(solution)/shard_map/add | solution.py:78
  48.3 2.5 multiply_add_fusion.19
  52.2 7.4 %multiply_add_fusion.17 = (f32[1,16384]{1,0:T(1,128)S(1)}, f32[1,16384]{1,0:T(1,128)S(1)}, f32[1,16384]{1,0:T(1,128)S(1)}, f32[1,16384]{1,0:T(1,128)S(1)}) fusion(f32[]{:T(128)} %bitcast.39, f32[]{:T(128)} %bitcast.35, f32[]{:T(128)} %bitcast.42, f32[3,16384]{1,0:T(4,128)} %param.10, f32[]{:T(128)} %bitcast.41, f32[]{:T(128)} %bitcast.40, f32[]{:T(128)S(6)} %neg.17, ...), kind=kLoop, calls=%fused_computation.61 | loop fusion | flops 327680 | bytes 458792 | tf_op jit(solution)/shard_map/add | solution.py:78
  59.6 7.2 %multiply_add_fusion.16 = (f32[1,16384]{1,0:T(1,128)S(1)}, f32[1,16384]{1,0:T(1,128)S(1)}, f32[1,16384]{1,0:T(1,128)S(1)}, f32[1,16384]{1,0:T(1,128)S(1)}) fusion(f32[1,16384]{1,0:T(1,128)S(1)} %get-tuple-element.28, f32[1,16384]{1,0:T(1,128)S(1)} %get-tuple-element.29, f32[]{:T(128)} %bitcast.40, f32[]{:T(128)} %bitcast.36, f32[]{:T(128)} %bitcast.37, ...), kind=kLoop, calls=%fused_computation.60 | loop fusion | flops 294912 | bytes 655400 | tf_op jit(solution)/shard_map/add | solution.py:78
  66.8 2.5 multiply_add_fusion.13
  70.7 7.4 %multiply_add_fusion.11 = (f32[1,16384]{1,0:T(1,128)S(1)}, f32[1,16384]{1,0:T(1,128)S(1)}, f32[1,16384]{1,0:T(1,128)S(1)}, f32[1,16384]{1,0:T(1,128)S(1)}) fusion(f32[]{:T(128)} %bitcast.58, f32[]{:T(128)} %bitcast.54, f32[]{:T(128)} %bitcast.61, f32[3,16384]{1,0:T(4,128)} %param.10, f32[]{:T(128)} %bitcast.60, f32[]{:T(128)} %bitcast.59, f32[]{:T(128)S(6)} %neg.18, ...), kind=kLoop, calls=%fused_computation.55 | loop fusion | flops 327680 | bytes 458792 | tf_op jit(solution)/shard_map/add | solution.py:78
  78.1 7.4 %multiply_add_fusion.10 = (f32[1,16384]{1,0:T(1,128)S(1)}, f32[1,16384]{1,0:T(1,128)S(1)}, f32[1,16384]{1,0:T(1,128)S(1)}, f32[1,16384]{1,0:T(1,128)S(1)}) fusion(f32[1,16384]{1,0:T(1,128)S(1)} %get-tuple-element.34, f32[1,16384]{1,0:T(1,128)S(1)} %get-tuple-element.35, f32[]{:T(128)} %bitcast.59, f32[]{:T(128)} %bitcast.55, f32[]{:T(128)} %bitcast.56, ...), kind=kLoop, calls=%fused_computation.54 | loop fusion | flops 294912 | bytes 655400 | tf_op jit(solution)/shard_map/add | solution.py:78
  85.5 2.6 multiply_add_fusion.7
  89.5 7.4 %multiply_add_fusion.5 = (f32[1,16384]{1,0:T(1,128)S(1)}, f32[1,16384]{1,0:T(1,128)S(1)}, f32[1,16384]{1,0:T(1,128)S(1)}, f32[1,16384]{1,0:T(1,128)S(1)}) fusion(f32[]{:T(128)} %bitcast.77, f32[]{:T(128)} %bitcast.73, f32[]{:T(128)} %bitcast.80, f32[3,16384]{1,0:T(4,128)} %param.10, f32[]{:T(128)} %bitcast.79, f32[]{:T(128)} %bitcast.78, f32[]{:T(128)S(6)} %neg.19, ...), kind=kLoop, calls=%fused_computation.49 | loop fusion | flops 327680 | bytes 458792 | tf_op jit(solution)/shard_map/add | solution.py:78
  96.8 7.4 %multiply_add_fusion.4 = (f32[1,16384]{1,0:T(1,128)S(1)}, f32[1,16384]{1,0:T(1,128)S(1)}, f32[1,16384]{1,0:T(1,128)S(1)}, f32[1,16384]{1,0:T(1,128)S(1)}) fusion(f32[1,16384]{1,0:T(1,128)S(1)} %get-tuple-element.40, f32[1,16384]{1,0:T(1,128)S(1)} %get-tuple-element.41, f32[]{:T(128)} %bitcast.78, f32[]{:T(128)} %bitcast.74, f32[]{:T(128)} %bitcast.75, ...), kind=kLoop, calls=%fused_computation.48 | loop fusion | flops 294912 | bytes 655400 | tf_op jit(solution)/shard_map/add | solution.py:78
  104.2 2.6 multiply_add_fusion.1
  106.8 1.8 slice_convert_fusion.3
  108.6 0.8 fusion.7
  109.4 0.8 add_sqrt_fusion.3
  110.2 1.8 multiply_maximum_fusion
  112.0 1.5 broadcast_in_dim.24
  113.5 5.3 %all-to-all-start = ((f32[8,1,32768]{2,1,0:T(1,128)}), f32[8,1,32768]{2,1,0:T(1,128)S(1)}, u32[]{:S(2)}, u32[]{:S(2)}) async-start(f32[8,1,32768]{2,1,0:T(1,128)} %broadcast_in_dim.24), calls=%async_computation | async-start | bytes 2097152 | tf_op jit(solution)/shard_map/all_to_all | solution.py:17
  122.2 0.7 add_minimum_fusion
  123.1 0.7 fusion.2
  123.8 1.4 compare_select_fusion.1
  125.2 8.5 %all-to-all-done = f32[8,1,32768]{2,1,0:T(1,128)S(1)} async-done(((f32[8,1,32768]{2,1,0:T(1,128)}), f32[8,1,32768]{2,1,0:T(1,128)S(1)}, u32[]{:S(2)}, u32[]{:S(2)}) %all-to-all-start) | async-done | bytes 1048608 | tf_op jit(solution)/shard_map/all_to_all | solution.py:17
  133.8 9.7 %all-to-all-start.2 = ((s32[1,32,4]{2,0,1:T(1,128)}), s32[1,32,4]{2,0,1:T(1,128)S(1)}, u32[]{:S(2)}, u32[]{:S(2)}) async-start(s32[1,32,4]{2,0,1:T(1,128)} %compare_select_fusion.1), calls=%async_computation.2 | async-start | bytes 32768 | tf_op jit(solution)/shard_map/all_to_all | solution.py:142
  143.5 0.8 reduce_max.9
  144.3 21.5 %concatenate.8 = f32[61,16384]{1,0:T(8,128)} concatenate(f32[3,16384]{1,0:T(4,128)S(1)} %copy-done.1, f32[3,16384]{1,0:T(4,128)S(1)} %copy-done.3, f32[4,16384]{1,0:T(4,128)S(1)} %copy-done.2, f32[49,16384]{1,0:T(8,128)} %param.13, f32[1,16384]{1,0:T(1,128)S(1)} %bitcast.259, f32[1,16384]{1,0:T(1,128)S(1)} %bitcast.261), dimensions={0} | concatenate | bytes 7995392 | tf_op jit(solution)/shard_map/concatenate | solution.py:109
  165.8 6.9 %copy.102 = f32[16384,61]{1,0:T(8,128)} copy(f32[16384,61]{0,1:T(8,128)} %bitcast.255) | data formatting | bytes 7995392 | tf_op jit(solution)/shard_map/concatenate | solution.py:109
  172.7 44.3 %scatter_custom_fusion = f32[61,16384]{0,1:T(8,128)} fusion(s32[16384]{0:T(1024)} %get-tuple-element.78, f32[16384,61]{1,0:T(8,128)} %copy.102, f32[]{:T(128)} %constant.32.clone.1), kind=kCustom, calls=%fused_computation.3 | custom fusion | bytes 3998208 | tf_op jit(solution)/shard_map/scatter | solution.py:121
  217.1 7.7 %gather_fusion = f32[128,61,128]{1,2,0:T(8,128)} fusion(f32[61,128,128]{0,2,1:T(8,128)} %bitcast.254, s32[1024]{0:T(1024)S(1)} %pad_clamp_fusion), kind=kCustom, calls=%fused_computation | custom fusion | bytes 7995904 | tf_op jit(solution)/shard_map/gather | solution.py:130
  224.8 1.4 dynamic-slice_multiply_fusion
  226.6 2.3 reshape.640
  229.0 9.1 %all-to-all-start.3 = ((f32[32,1,3904]{2,1,0:T(1,128)}), f32[32,1,3904]{2,1,0:T(1,128)S(1)}, u32[]{:S(2)}, u32[]{:S(2)}) async-start(f32[32,1,3904]{2,1,0:T(1,128)} %reshape.640), calls=%async_computation.3 | async-start | bytes 1015808 | tf_op jit(solution)/shard_map/all_to_all | solution.py:11
  239.4 11.3 %all-to-all-done.3 = f32[32,1,3904]{2,1,0:T(1,128)S(1)} async-done(((f32[32,1,3904]{2,1,0:T(1,128)}), f32[32,1,3904]{2,1,0:T(1,128)S(1)}, u32[]{:S(2)}, u32[]{:S(2)}) %all-to-all-start.3) | async-done | bytes 499744 | tf_op jit(solution)/shard_map/all_to_all | solution.py:11
  251.2 1.8 reduce.9
  253.1 1.5 reshape.641
  254.7 4.5 %scatter_fusion = f32[61,128,16]{0,2,1:T(8,128)S(1)} fusion(f32[61,128,16]{0,2,1:T(8,128)S(1)} %broadcast_in_dim.44, s32[128]{0:T(128)S(1)} %fusion.4, f32[128,61,16]{1,2,0:T(8,128)S(1)} %bitcast.253), kind=kCustom, calls=%fused_computation.2 | custom fusion | bytes 1499648 | tf_op jit(solution)/shard_map/scatter | solution.py:148
  259.2 1.0 copy-done
  260.8 16.9 %all_to_all.31 = f32[32,1,1]{2,1,0:T(1,128)S(1)} all-to-all(f32[32,1,1]{2,1,0:T(1,128)S(1)} %broadcast_in_dim.51), channel_id=1, replica_groups=mesh['view'=8,'gauss'=32] {'gauss'}, dimensions={0} | all-to-all | bytes 256 | tf_op jit(solution)/shard_map/all_to_all | solution.py:17
  279.0 0.8 pad_maximum_fusion.1
  279.8 32.5 %all-gather.2.cloned.1.call-done = f32[61,128,128]{0,2,1:T(8,128)} async-done(((f32[61,128,16]{0,2,1:T(8,128)}), f32[61,128,128]{0,2,1:T(8,128)}) %all-gather.2.cloned.1.call-update) | async-done | bytes 3997712 | tf_op jit(solution)/shard_map/all_gather | solution.py:150
  312.3 6.8 %copy.104 = f32[61,16384]{1,0:T(8,128)} copy(f32[61,16384]{0,1:T(8,128)} %bitcast.256) | data formatting | bytes 7995392
  (90 shorter events, 9.6 us)
Async XLA Ops:
  7.2 101.4 %copy-start.3 = (f32[3,16384]{1,0:T(4,128)S(1)}, f32[3,16384]{1,0:T(4,128)}, u32[]{:S(2)}) copy-start(f32[3,16384]{1,0:T(4,128)} %param.11) | copy-start | bytes 589828
  7.2 102.2 %copy-start.4 = (f32[4,2,16384]{2,1,0:T(2,128)S(1)}, f32[4,2,16384]{2,1,0:T(2,128)}, u32[]{:S(2)}) copy-start(f32[4,2,16384]{2,1,0:T(2,128)} %param.14) | copy-start | bytes 1572868
  12.2 99.8 %all-to-all-start.1 = ((s32[32,1,1]{2,1,0:T(1,128)}), s32[32,1,1]{2,1,0:T(1,128)S(1)}, u32[]{:S(2)}, u32[]{:S(2)}) async-start(s32[32,1,1]{2,1,0:T(1,128)} %broadcast_in_dim.45), calls=%async_computation.1 | async-start | bytes 32768 | tf_op jit(solution)/shard_map/all_to_all | solution.py:17
  24.2 120.0 %copy-start.1 = (f32[3,16384]{1,0:T(4,128)S(1)}, f32[3,16384]{1,0:T(4,128)}, u32[]{:S(2)}) copy-start(f32[3,16384]{1,0:T(4,128)} %param.10) | copy-start | bytes 589828
  24.2 120.0 %copy-start.2 = (f32[4,16384]{1,0:T(4,128)S(1)}, f32[4,16384]{1,0:T(4,128)}, u32[]{:S(2)}) copy-start(f32[4,16384]{1,0:T(4,128)} %param.12) | copy-start | bytes 786436
  113.5 20.2 %all-to-all-start = ((f32[8,1,32768]{2,1,0:T(1,128)}), f32[8,1,32768]{2,1,0:T(1,128)S(1)}, u32[]{:S(2)}, u32[]{:S(2)}) async-start(f32[8,1,32768]{2,1,0:T(1,128)} %broadcast_in_dim.24), calls=%async_computation | async-start | bytes 2097152 | tf_op jit(solution)/shard_map/all_to_all | solution.py:17
  133.8 95.2 %all-to-all-start.2 = ((s32[1,32,4]{2,0,1:T(1,128)}), s32[1,32,4]{2,0,1:T(1,128)S(1)}, u32[]{:S(2)}, u32[]{:S(2)}) async-start(s32[1,32,4]{2,0,1:T(1,128)} %compare_select_fusion.1), calls=%async_computation.2 | async-start | bytes 32768 | tf_op jit(solution)/shard_map/all_to_all | solution.py:142
  229.0 21.8 %all-to-all-start.3 = ((f32[32,1,3904]{2,1,0:T(1,128)}), f32[32,1,3904]{2,1,0:T(1,128)S(1)}, u32[]{:S(2)}, u32[]{:S(2)}) async-start(f32[32,1,3904]{2,1,0:T(1,128)} %reshape.640), calls=%async_computation.3 | async-start | bytes 1015808 | tf_op jit(solution)/shard_map/all_to_all | solution.py:11
  238.0 74.3 %all-gather.2.cloned.1.call-start = ((), (), s32[]{:S(2)}) async-start(), calls=%async_computation.5 | async-start | bytes 9437184 | tf_op jit(solution)/shard_map/all_gather | solution.py:150
  259.2 1.0 copy-start
Sparse Core Ops, SparseCore 0:
  260.3 51.9 all-gather.1
